TPU v7x, 32 devices: a whole 2x2x4 slice. The times are simulated.
32 devices in a mesh: dp: 4 (over y, core), expert: 4 (over z), tensor: 2 (over x).
Axes of the slice: x: 2, y: 2, z: 4, core: 2. Of those that a mesh axis runs over, the one named last changes fastest.
Arguments:
- tokens: bfloat16 [256, 3072], P(('dp', 'expert')), may hold values from -45 to 45
- cotangent: bfloat16 [256, 3072], P(('dp', 'expert')), may hold values from -6 to 6
- gain: float32 [3072], replicated, may hold values from 0.5 to 1.5
- w_router: bfloat16 [3072, 4], replicated, may hold values from -0.109375 to 0.109375
- w_gate: bfloat16 [4, 3072, 9216], P('expert', None, 'tensor'), may hold values from -0.109375 to 0.109375
- w_up: bfloat16 [4, 3072, 9216], P('expert', None, 'tensor'), may hold values from -0.109375 to 0.109375
- w_down: bfloat16 [4, 9216, 3072], P('expert', 'tensor'), may hold values from -0.0625 to 0.0625
- expert_ids: int32 [256, 2], P(('dp', 'expert')), may hold values from 0 to 3, as said below
- slots: int32 [256, 2], P(('dp', 'expert')), may hold values from 0 to 7, as said below
Outputs:
- mixed: bfloat16 [256, 3072], P(('dp', 'expert'))
- grad_tokens: bfloat16 [256, 3072], P(('dp', 'expert'))
- grad_router: float32 [3072, 4], replicated
- grad_gain: float32 [3072], replicated
Inputs may be any that keep to these rules, and one draw needn't show every extreme that they name: `expert_ids`: within each aligned block of 16 rows (one group), every expert is named exactly 8 times, and a row's two ids differ. Within each aligned block of 16 rows, the choices naming one expert hold its slots 0 to 7, each once.
All inputs are finite; a program needn't handle non-finite values.
Results may differ from a plain program's by a relative error of at most 0.0095.
Values may be sent and summed in bfloat16 or wider, within the bound.
No kernel may reach another device: no remote copies, remote signals or barrier semaphores. Data moves between devices by JAX's collectives and lax.ppermute only.
A program may use at most 128 MiB of HBM per device.

v0:
```python
import jax
import jax.numpy as jnp
from jax import lax
from jax.sharding import PartitionSpec as P

epsilon = 1e-05


def pack_rows(select, values):
    return jnp.einsum("tcr,tcd->rd", select, values, preferred_element_type=jnp.float32).astype(
        jnp.bfloat16
    )


def repeat_blocks(packed, experts, copies):
    feature_width = packed.shape[1]
    blocks = packed.reshape(experts, 1, -1, feature_width)
    blocks = jnp.broadcast_to(blocks, (experts, copies, blocks.shape[2], feature_width))
    return blocks.reshape(experts * copies, -1, feature_width)


def to_experts(packed, experts, copies):
    arrived = lax.all_to_all(
        repeat_blocks(packed, experts, copies), "expert", split_axis=0, concat_axis=0, tiled=True
    )
    return arrived.reshape(-1, packed.shape[1])


def from_experts(partial_value, row_index, experts, copies):
    partial_value = lax.psum_scatter(
        partial_value.astype(jnp.bfloat16), "tensor", scatter_dimension=1, tiled=True
    ).astype(jnp.float32)
    feature_width = partial_value.shape[1]
    returned_rows = lax.all_to_all(
        partial_value.reshape(experts * copies, -1, feature_width),
        "expert",
        split_axis=0,
        concat_axis=0,
        tiled=True,
    )
    summed = jnp.sum(returned_rows.reshape(experts, copies, -1, feature_width), axis=1).reshape(
        -1, feature_width
    )
    picked = summed[row_index]
    picked = lax.all_gather(picked.astype(jnp.bfloat16), "tensor", axis=2, tiled=True).astype(
        picked.dtype
    )
    return picked


def shards(tokens, cotangent, gain, w_router, w_gate, w_up, w_down, expert_ids, slots):
    experts = w_router.shape[1]
    copies = lax.axis_size("expert") // experts
    token_count = tokens.shape[0]
    capacity = 2 * token_count // experts
    floats = tokens.astype(jnp.float32)
    inv_rms = lax.rsqrt(jnp.mean(floats * floats, axis=1, keepdims=True) + epsilon)
    normed = (floats * inv_rms * gain).astype(jnp.bfloat16)
    logits = jnp.dot(normed, w_router, preferred_element_type=jnp.float32)
    chosen_logits = jnp.take_along_axis(logits, expert_ids, axis=1)
    first_prob = jax.nn.sigmoid(chosen_logits[:, 0] - chosen_logits[:, 1])
    pair_probs = jnp.stack([first_prob, 1.0 - first_prob], axis=1)
    row_index = expert_ids * capacity + slots
    select = (
        row_index[:, :, None] == jnp.arange(experts * capacity, dtype=jnp.int32)[None, None, :]
    ).astype(jnp.bfloat16)
    feature_width = tokens.shape[1]
    inputs = to_experts(
        pack_rows(select, jnp.broadcast_to(normed[:, None, :], (token_count, 2, feature_width))),
        experts,
        copies,
    )
    gate_matrix = w_gate[0]
    up_matrix = w_up[0]
    down_matrix = w_down[0]
    gate_pre = jnp.dot(inputs, gate_matrix, preferred_element_type=jnp.float32)
    up_pre = jnp.dot(inputs, up_matrix, preferred_element_type=jnp.float32)
    activated = (jax.nn.silu(gate_pre) * up_pre).astype(jnp.bfloat16)
    chosen = from_experts(
        jnp.dot(activated, down_matrix, preferred_element_type=jnp.float32),
        row_index,
        experts,
        copies,
    )
    mixed = (floats + jnp.sum(pair_probs[:, :, None] * chosen, axis=1)).astype(jnp.bfloat16)
    upstream = cotangent.astype(jnp.float32)
    sent_grads = (pair_probs[:, :, None] * upstream[:, None, :]).astype(jnp.bfloat16)
    grad_outputs = to_experts(pack_rows(select, sent_grads), experts, copies)
    grad_act = jnp.dot(grad_outputs, down_matrix.T, preferred_element_type=jnp.float32)
    sigmoid_gate = jax.nn.sigmoid(gate_pre)
    grad_gate = (grad_act * up_pre * sigmoid_gate * (1.0 + gate_pre * (1.0 - sigmoid_gate))).astype(
        jnp.bfloat16
    )
    grad_up = (grad_act * jax.nn.silu(gate_pre)).astype(jnp.bfloat16)
    grad_inputs = jnp.dot(grad_gate, gate_matrix.T, preferred_element_type=jnp.float32) + jnp.dot(
        grad_up, up_matrix.T, preferred_element_type=jnp.float32
    )
    grad_mixture = jnp.sum(from_experts(grad_inputs, row_index, experts, copies), axis=1)
    grad_probs = jnp.sum(upstream[:, None, :] * chosen, axis=2)
    grad_first = first_prob * (1.0 - first_prob) * (grad_probs[:, 0] - grad_probs[:, 1])
    columns = jnp.arange(experts, dtype=jnp.int32)[None, :]
    grad_logits = grad_first[:, None] * (
        (expert_ids[:, 0:1] == columns).astype(jnp.float32)
        - (expert_ids[:, 1:2] == columns).astype(jnp.float32)
    )
    grad_normed = grad_mixture + jnp.dot(
        grad_logits, w_router.astype(jnp.float32).T, precision=lax.Precision.HIGHEST
    )
    router_part = jnp.dot(
        normed.astype(jnp.float32).T, grad_logits, precision=lax.Precision.HIGHEST
    )
    gain_part = jnp.sum(grad_normed * floats * inv_rms, axis=0)
    grad_router, grad_gain = lax.psum((router_part, gain_part), ("dp", "expert"))
    grad_scaled = grad_normed * gain
    cubed = inv_rms * inv_rms * inv_rms
    grad_tokens = (
        upstream
        + inv_rms * grad_scaled
        - floats * cubed * jnp.mean(grad_scaled * floats, axis=1, keepdims=True)
    ).astype(jnp.bfloat16)
    return (mixed, grad_tokens, grad_router, grad_gain)


def solution(mesh):
    return jax.shard_map(
        shards,
        mesh=mesh,
        in_specs=(
            P(("dp", "expert"), None),
            P(("dp", "expert"), None),
            P(),
            P(),
            P("expert", None, "tensor"),
            P("expert", None, "tensor"),
            P("expert", "tensor", None),
            P(("dp", "expert"), None),
            P(("dp", "expert"), None),
        ),
        out_specs=(P(("dp", "expert"), None), P(("dp", "expert"), None), P(), P()),
        check_vma=False,
    )
```

profile of v0, /device:TPU:0, one launch (start us, length us, event | category | flops | bytes accessed | tf_op | source)
XLA Modules:
  0.0 204.1 jit_solution(13842822642820997463)
XLA Ops:
  7.2 0.0 copy-start
  7.2 1.0 fusion.29
  8.2 0.7 compare_select_fusion
  8.9 1.0 fusion.31
  9.9 1.0 fusion.24
  10.9 6.3 %all-to-all-start = ((bf16[4,8,3072]{2,1,0:T(8,128)(2,1)}), bf16[4,8,3072]{2,1,0:T(8,128)(2,1)S(1)}, u32[]{:S(2)}, u32[]{:S(2)}) async-start(bf16[4,8,3072]{2,1,0:T(8,128)(2,1)} %fusion.24), calls=%async_computation | async-start | bytes 393216 | tf_op jit(solution)/shard_map/all_to_all | solution.py:23
  17.3 0.7 bitcast_or_fusion
  17.9 0.1 copy.39
  18.0 0.1 reshape.101
  18.1 0.1 fusion.59
  18.3 0.8 gather_fusion.2
  19.0 0.1 reshape.104
  19.1 0.1 copy.40
  19.2 0.7 and_select_fusion
  19.9 0.9 convert_element_type.70
  20.8 1.0 fusion.23
  21.8 2.9 %all-to-all-done = bf16[4,8,3072]{2,1,0:T(8,128)(2,1)S(1)} async-done(((bf16[4,8,3072]{2,1,0:T(8,128)(2,1)}), bf16[4,8,3072]{2,1,0:T(8,128)(2,1)S(1)}, u32[]{:S(2)}, u32[]{:S(2)}) %all-to-all-start) | async-done | bytes 196640 | tf_op jit(solution)/shard_map/all_to_all | solution.py:23
  24.8 3.4 %all-to-all-start.2 = ((bf16[4,8,3072]{2,1,0:T(8,128)(2,1)}), bf16[4,8,3072]{2,1,0:T(8,128)(2,1)S(1)}, u32[]{:S(2)}, u32[]{:S(2)}) async-start(bf16[4,8,3072]{2,1,0:T(8,128)(2,1)} %fusion.23), calls=%async_computation.3 | async-start | bytes 393216 | tf_op jit(solution)/shard_map/all_to_all | solution.py:23
  28.1 0.0 reduce-scatter.3.cloned.1.call-start
  28.2 11.5 %fusion.10 = f32[32,4608]{1,0:T(8,128)S(1)} fusion(bf16[1,3072,4608]{2,1,0:T(8,128)(2,1)} %param.13, bf16[4,8,3072]{2,1,0:T(8,128)(2,1)S(1)} %all-to-all-done), kind=kOutput, calls=%fused_computation.13 | convolution fusion | flops 905969664 | bytes 29097984 | tf_op jit(solution)/shard_map/dot_general | solution.py:76
  39.7 11.5 %fusion.6 = f32[32,4608]{1,0:T(8,128)S(1)} fusion(bf16[1,3072,4608]{2,1,0:T(8,128)(2,1)} %param.14, bf16[4,8,3072]{2,1,0:T(8,128)(2,1)S(1)} %all-to-all-done), kind=kOutput, calls=%fused_computation.9 | convolution fusion | flops 905969664 | bytes 29097984 | tf_op jit(solution)/shard_map/dot_general | solution.py:77
  51.2 12.3 %fusion.20 = bf16[32,3072]{1,0:T(8,128)(2,1)} fusion(bf16[1,4608,3072]{2,1,0:T(8,128)(2,1)} %param.15, f32[32,4608]{1,0:T(8,128)S(1)} %fusion.6, f32[32,4608]{1,0:T(8,128)S(1)} %fusion.10), kind=kOutput, calls=%fused_computation.21 | convolution fusion | flops 906952704 | bytes 29687808 | tf_op jit(solution)/shard_map/dot_general | solution.py:80
  63.6 0.0 reduce-scatter.3.cloned.1.call-update
  63.6 0.2 reduce-scatter.5.cloned.1.call-start
  63.8 0.0 all-to-all-done.2
  63.8 13.6 %fusion = f32[32,4608]{1,0:T(8,128)S(1)} fusion(bf16[1,4608,3072]{2,1,0:T(8,128)(2,1)} %param.15, bf16[4,8,3072]{2,1,0:T(8,128)(2,1)S(1)} %all-to-all-done.2), kind=kOutput, calls=%fused_computation.3 | convolution fusion | flops 905969664 | bytes 29097984 | tf_op jit(solution)/shard_map/dot_general | solution.py:89
  77.4 13.5 %fusion.4 = f32[32,3072]{1,0:T(8,128)S(1)} fusion(bf16[1,3072,4608]{2,1,0:T(8,128)(2,1)} %param.14, f32[32,4608]{1,0:T(8,128)S(1)} %fusion, f32[32,4608]{1,0:T(8,128)S(1)} %fusion.10), kind=kOutput, calls=%fused_computation.7 | convolution fusion | flops 906854400 | bytes 29884416 | tf_op jit(solution)/shard_map/dot_general | solution.py:95
  90.9 0.0 copy-start.1
  90.9 0.0 copy-start.3
  90.9 0.0 copy-start.2
  90.9 14.3 %fusion.15 = bf16[32,3072]{1,0:T(8,128)(2,1)} fusion(f32[32,3072]{1,0:T(8,128)S(1)} %fusion.4, bf16[1,3072,4608]{2,1,0:T(8,128)(2,1)} %param.13, f32[32,4608]{1,0:T(8,128)S(1)} %fusion.10, f32[32,4608]{1,0:T(8,128)S(1)} %fusion, f32[32,4608]{1,0:T(8,128)S(1)} %fusion.6), kind=kOutput, calls=%fused_computation.18 | convolution fusion | flops 907640832 | bytes 30670848 | tf_op jit(solution)/shard_map/dot_general | solution.py:95
  105.2 0.0 reduce-scatter.5.cloned.1.call-update
  105.2 0.0 reduce-scatter.3.cloned.1.call-done
  105.2 5.0 %all-to-all-start.1 = ((bf16[4,8,1536]{2,1,0:T(8,128)(2,1)}), bf16[4,8,1536]{2,1,0:T(8,128)(2,1)S(1)}, u32[]{:S(2)}, u32[]{:S(2)}) async-start(bf16[4,8,1536]{2,1,0:T(8,128)(2,1)} %bitcast.72), calls=%async_computation.2 | async-start | bytes 196608 | tf_op jit(solution)/shard_map/all_to_all | solution.py:34
  110.3 0.1 copy.41
  110.4 0.1 reshape.87
  110.5 7.3 %reduce-scatter.5.cloned.1.call-done = bf16[32,1536]{1,0:T(8,128)(2,1)} async-done(((bf16[32,3072]{1,0:T(8,128)(2,1)}), bf16[32,1536]{1,0:T(8,128)(2,1)}) %reduce-scatter.5.cloned.1.call-update) | async-done | bytes 98320 | tf_op jit(solution)/shard_map/reduce_scatter | solution.py:30
  117.8 4.6 %all-to-all-start.3 = ((bf16[4,8,1536]{2,1,0:T(8,128)(2,1)}), bf16[4,8,1536]{2,1,0:T(8,128)(2,1)S(1)}, u32[]{:S(2)}, u32[]{:S(2)}) async-start(bf16[4,8,1536]{2,1,0:T(8,128)(2,1)} %bitcast.71), calls=%async_computation.5 | async-start | bytes 196608 | tf_op jit(solution)/shard_map/all_to_all | solution.py:34
  122.4 0.6 gather_fusion
  123.1 5.3 %all_gather.6 = bf16[16,2,3072]{2,0,1:T(8,128)(2,1)S(1)} all-gather(bf16[16,2,1536]{2,0,1:T(8,128)(2,1)S(1)} %copy.42), channel_id=1, replica_groups=mesh['dp'=4,'expert'=4,'tensor'=2] {'tensor'}, dimensions={2}, use_global_device_ids=true | all-gather | bytes 294912 | tf_op jit(solution)/shard_map/all_gather | solution.py:45
  128.4 0.1 fusion.27
  128.5 0.6 gather_fusion.1
  129.2 5.3 %all_gather.7 = bf16[16,2,3072]{2,1,0:T(2,128)(2,1)S(1)} all-gather(bf16[16,2,1536]{2,1,0:T(2,128)(2,1)S(1)} %reshape.112), channel_id=1, replica_groups=mesh['dp'=4,'expert'=4,'tensor'=2] {'tensor'}, dimensions={2}, use_global_device_ids=true | all-gather | bytes 294912 | tf_op jit(solution)/shard_map/all_gather | solution.py:45
  134.5 0.5 convert_reduce_fusion
  135.0 0.3 fusion.47
  135.4 0.5 fusion.38
  135.8 60.6 %all-reduce = (f32[3072,4]{0,1:T(4,128)}, f32[3072]{0:T(1024)}) all-reduce(f32[3072,4]{0,1:T(4,128)S(1)} %fusion.47, f32[3072]{0:T(1024)S(1)} %get-tuple-element.4), channel_id=1, replica_groups=mesh['dp'=4,'expert'=4,'tensor'=2] {'dp','expert'}, use_global_device_ids=true, to_apply=%region_7.8 | all-reduce | flops 15360 | bytes 122880 | tf_op jit(solution)/shard_map/psum | solution.py:113
  196.5 0.8 fusion.35
  (18 shorter events, 0.2 us)
Async XLA Ops:
  7.2 11.0 %copy-start = (bf16[3072,4]{0,1:T(4,128)(2,1)S(1)}, bf16[3072,4]{0,1:T(4,128)(2,1)}, u32[]{:S(2)}) copy-start(bf16[3072,4]{0,1:T(4,128)(2,1)} %param.12) | copy-start | bytes 73732
  10.9 13.9 %all-to-all-start = ((bf16[4,8,3072]{2,1,0:T(8,128)(2,1)}), bf16[4,8,3072]{2,1,0:T(8,128)(2,1)S(1)}, u32[]{:S(2)}, u32[]{:S(2)}) async-start(bf16[4,8,3072]{2,1,0:T(8,128)(2,1)} %fusion.24), calls=%async_computation | async-start | bytes 393216 | tf_op jit(solution)/shard_map/all_to_all | solution.py:23
  24.8 39.0 %all-to-all-start.2 = ((bf16[4,8,3072]{2,1,0:T(8,128)(2,1)}), bf16[4,8,3072]{2,1,0:T(8,128)(2,1)S(1)}, u32[]{:S(2)}, u32[]{:S(2)}) async-start(bf16[4,8,3072]{2,1,0:T(8,128)(2,1)} %fusion.23), calls=%async_computation.3 | async-start | bytes 393216 | tf_op jit(solution)/shard_map/all_to_all | solution.py:23
  28.1 77.1 %reduce-scatter.3.cloned.1.call-start = ((), (), s32[]{:S(2)}) async-start(), calls=%async_computation.6 | async-start | bytes 294912 | tf_op jit(solution)/shard_map/reduce_scatter | solution.py:30
  63.6 54.2 %reduce-scatter.5.cloned.1.call-start = ((), (), s32[]{:S(2)}) async-start(), calls=%async_computation.7 | async-start | bytes 294912 | tf_op jit(solution)/shard_map/reduce_scatter | solution.py:30
  90.9 19.4 %copy-start.4 = (s32[16,2]{0,1:T(2,128)S(1)}, s32[16,2]{0,1:T(2,128)}, u32[]{:S(2)}) copy-start(s32[16,2]{0,1:T(2,128)} %param.16) | copy-start | bytes 388
  90.9 44.5 %copy-start.1 = (bf16[16,3072]{1,0:T(8,128)(2,1)S(1)}, bf16[16,3072]{1,0:T(8,128)(2,1)}, u32[]{:S(2)}) copy-start(bf16[16,3072]{1,0:T(8,128)(2,1)} %param.9) | copy-start | bytes 294916
  90.9 44.5 %copy-start.3 = (f32[3072]{0:T(1024)S(1)}, f32[3072]{0:T(1024)}, u32[]{:S(2)}) copy-start(f32[3072]{0:T(1024)} %param.11) | copy-start | bytes 36868
  90.9 105.5 %copy-start.2 = (bf16[16,3072]{1,0:T(8,128)(2,1)S(1)}, bf16[16,3072]{1,0:T(8,128)(2,1)}, u32[]{:S(2)}) copy-start(bf16[16,3072]{1,0:T(8,128)(2,1)} %param.10) | copy-start | bytes 294916
  105.2 12.5 %all-to-all-start.1 = ((bf16[4,8,1536]{2,1,0:T(8,128)(2,1)}), bf16[4,8,1536]{2,1,0:T(8,128)(2,1)S(1)}, u32[]{:S(2)}, u32[]{:S(2)}) async-start(bf16[4,8,1536]{2,1,0:T(8,128)(2,1)} %bitcast.72), calls=%async_computation.2 | async-start | bytes 196608 | tf_op jit(solution)/shard_map/all_to_all | solution.py:34
  117.8 10.8 %all-to-all-start.3 = ((bf16[4,8,1536]{2,1,0:T(8,128)(2,1)}), bf16[4,8,1536]{2,1,0:T(8,128)(2,1)S(1)}, u32[]{:S(2)}, u32[]{:S(2)}) async-start(bf16[4,8,1536]{2,1,0:T(8,128)(2,1)} %bitcast.71), calls=%async_computation.5 | async-start | bytes 196608 | tf_op jit(solution)/shard_map/all_to_all | solution.py:34
Sparse Core Ops, SparseCore 0:
  63.7 12.3 reduce-scatter.2
  105.3 12.3 reduce-scatter.4
where the time goes:
time: 205 us; the launch traced here: 204 us
  matrix products  79.6 us (39%)
  blocking collectives  71.2 us (35%)
  starting transfers between devices  19.6 us (10%)
  between operations  14.2 us (7%)
  waiting for transfers between devices  10.3 us (5%)
  other arithmetic  6.49 us (3%)
  local copies, waits for them, and re-layouts  2.68 us (1%)
    psum x1, blocking collectives, shards(): lax.psum((router_part, gain_part), ('dp', 'expert'))  60.6 us
    dot_general x1, matrix products, shards(): jnp.dot(grad_gate, gate_matrix.T, preferred_element_type=jnp.float32)  14.3 us
    dot_general x1, matrix products, shards(): jnp.dot(grad_outputs, down_matrix.T, preferred_element_type=jnp.float32)  13.6 us
    dot_general x1, matrix products, shards(): jnp.dot(grad_up, up_matrix.T, preferred_element_type=jnp.float32)  13.5 us
    dot_general x1, matrix products, shards(): jnp.dot(activated, down_matrix, preferred_element_type=jnp.float32)  12.3 us
    dot_general x1, matrix products, shards(): gate_pre = jnp.dot(inputs, gate_matrix, preferred_element_type=jnp.float32)  11.5 us
    dot_general x1, matrix products, shards(): up_pre = jnp.dot(inputs, up_matrix, preferred_element_type=jnp.float32)  11.5 us
    all_gather x2, blocking collectives, from_experts(): lax.all_gather(picked.astype(jnp.bfloat16), 'tensor', axis=2, tiled=True)  10.6 us
  transfers between devices with their start and end apart: 6, of which 2 were waited for; matrix products, arithmetic and copies ran while one was open for 40% of the time, Pallas kernels for 0%

commit v1 on v0

--- a/solution.py
+++ b/solution.py
@@ -110,7 +110,7 @@
         normed.astype(jnp.float32).T, grad_logits, precision=lax.Precision.HIGHEST
     )
     gain_part = jnp.sum(grad_normed * floats * inv_rms, axis=0)
-    grad_router, grad_gain = lax.psum((router_part, gain_part), ("dp", "expert"))
+    grad_router, grad_gain = lax.psum(lax.psum((router_part, gain_part), "expert"), "dp")
     grad_scaled = grad_normed * gain
     cubed = inv_rms * inv_rms * inv_rms
     grad_tokens = (

time: 205 us -> 176 us (0.86)
  blocking collectives: 71.2 us -> 42 us
    psum x1 -> x2, blocking collectives: 60.6 us -> 31.4 us  [the longest x1 20.1 us: shards(): lax.psum((router_part, gain_part), 'expert')]
  transfers between devices with their start and end apart: 6 -> 6, of which waited for: 2 -> 2; matrix products, arithmetic and copies ran while one was open for 40% -> 47% of each run, Pallas kernels for 0% -> 0%
where the time goes in v1:
time: 176 us; the launch traced here: 175 us
  matrix products  79.6 us (45%)
  blocking collectives  42 us (24%)
  starting transfers between devices  19.6 us (11%)
  between operations  14.2 us (8%)
  waiting for transfers between devices  10.3 us (6%)
  other arithmetic  6.49 us (4%)
  local copies, waits for them, and re-layouts  2.68 us (2%)
    psum x1, blocking collectives, shards(): lax.psum((router_part, gain_part), 'expert')  20.1 us
    dot_general x1, matrix products, shards(): jnp.dot(grad_gate, gate_matrix.T, preferred_element_type=jnp.float32)  14.3 us
    dot_general x1, matrix products, shards(): jnp.dot(grad_outputs, down_matrix.T, preferred_element_type=jnp.float32)  13.6 us
    dot_general x1, matrix products, shards(): jnp.dot(grad_up, up_matrix.T, preferred_element_type=jnp.float32)  13.5 us
    dot_general x1, matrix products, shards(): jnp.dot(activated, down_matrix, preferred_element_type=jnp.float32)  12.3 us
    dot_general x1, matrix products, shards(): gate_pre = jnp.dot(inputs, gate_matrix, preferred_element_type=jnp.float32)  11.5 us
    dot_general x1, matrix products, shards(): up_pre = jnp.dot(inputs, up_matrix, preferred_element_type=jnp.float32)  11.5 us
    psum x1, blocking collectives, shards(): lax.psum(lax.psum((router_part, gain_part), 'expert'), 'dp')  11.3 us
  transfers between devices with their start and end apart: 6, of which 2 were waited for; matrix products, arithmetic and copies ran while one was open for 47% of the time, Pallas kernels for 0%

profile of v1, /device:TPU:0, one launch (start us, length us, event | category | flops | bytes accessed | tf_op | source)
XLA Modules:
  0.0 174.9 jit_solution(1627335754137936958)
XLA Ops:
  7.2 0.0 copy-start
  7.2 1.0 fusion.29
  8.2 0.7 compare_select_fusion
  8.9 1.0 fusion.31
  9.9 1.0 fusion.24
  10.9 6.3 %all-to-all-start = ((bf16[4,8,3072]{2,1,0:T(8,128)(2,1)}), bf16[4,8,3072]{2,1,0:T(8,128)(2,1)S(1)}, u32[]{:S(2)}, u32[]{:S(2)}) async-start(bf16[4,8,3072]{2,1,0:T(8,128)(2,1)} %fusion.24), calls=%async_computation | async-start | bytes 393216 | tf_op jit(solution)/shard_map/all_to_all | solution.py:23
  17.3 0.7 bitcast_or_fusion
  17.9 0.1 copy.39
  18.0 0.1 reshape.101
  18.1 0.1 fusion.59
  18.3 0.8 gather_fusion.2
  19.0 0.1 reshape.104
  19.1 0.1 copy.40
  19.2 0.7 and_select_fusion
  19.9 0.9 convert_element_type.70
  20.8 1.0 fusion.23
  21.8 2.9 %all-to-all-done = bf16[4,8,3072]{2,1,0:T(8,128)(2,1)S(1)} async-done(((bf16[4,8,3072]{2,1,0:T(8,128)(2,1)}), bf16[4,8,3072]{2,1,0:T(8,128)(2,1)S(1)}, u32[]{:S(2)}, u32[]{:S(2)}) %all-to-all-start) | async-done | bytes 196640 | tf_op jit(solution)/shard_map/all_to_all | solution.py:23
  24.8 3.4 %all-to-all-start.2 = ((bf16[4,8,3072]{2,1,0:T(8,128)(2,1)}), bf16[4,8,3072]{2,1,0:T(8,128)(2,1)S(1)}, u32[]{:S(2)}, u32[]{:S(2)}) async-start(bf16[4,8,3072]{2,1,0:T(8,128)(2,1)} %fusion.23), calls=%async_computation.3 | async-start | bytes 393216 | tf_op jit(solution)/shard_map/all_to_all | solution.py:23
  28.1 0.0 reduce-scatter.3.cloned.1.call-start
  28.2 11.5 %fusion.10 = f32[32,4608]{1,0:T(8,128)S(1)} fusion(bf16[1,3072,4608]{2,1,0:T(8,128)(2,1)} %param.13, bf16[4,8,3072]{2,1,0:T(8,128)(2,1)S(1)} %all-to-all-done), kind=kOutput, calls=%fused_computation.13 | convolution fusion | flops 905969664 | bytes 29097984 | tf_op jit(solution)/shard_map/dot_general | solution.py:76
  39.7 11.5 %fusion.6 = f32[32,4608]{1,0:T(8,128)S(1)} fusion(bf16[1,3072,4608]{2,1,0:T(8,128)(2,1)} %param.14, bf16[4,8,3072]{2,1,0:T(8,128)(2,1)S(1)} %all-to-all-done), kind=kOutput, calls=%fused_computation.9 | convolution fusion | flops 905969664 | bytes 29097984 | tf_op jit(solution)/shard_map/dot_general | solution.py:77
  51.2 12.3 %fusion.20 = bf16[32,3072]{1,0:T(8,128)(2,1)} fusion(bf16[1,4608,3072]{2,1,0:T(8,128)(2,1)} %param.15, f32[32,4608]{1,0:T(8,128)S(1)} %fusion.6, f32[32,4608]{1,0:T(8,128)S(1)} %fusion.10), kind=kOutput, calls=%fused_computation.21 | convolution fusion | flops 906952704 | bytes 29687808 | tf_op jit(solution)/shard_map/dot_general | solution.py:80
  63.6 0.0 reduce-scatter.3.cloned.1.call-update
  63.6 0.2 reduce-scatter.5.cloned.1.call-start
  63.8 13.6 %fusion = f32[32,4608]{1,0:T(8,128)S(1)} fusion(bf16[1,4608,3072]{2,1,0:T(8,128)(2,1)} %param.15, bf16[4,8,3072]{2,1,0:T(8,128)(2,1)S(1)} %all-to-all-done.2), kind=kOutput, calls=%fused_computation.3 | convolution fusion | flops 905969664 | bytes 29097984 | tf_op jit(solution)/shard_map/dot_general | solution.py:89
  77.4 13.5 %fusion.4 = f32[32,3072]{1,0:T(8,128)S(1)} fusion(bf16[1,3072,4608]{2,1,0:T(8,128)(2,1)} %param.14, f32[32,4608]{1,0:T(8,128)S(1)} %fusion, f32[32,4608]{1,0:T(8,128)S(1)} %fusion.10), kind=kOutput, calls=%fused_computation.7 | convolution fusion | flops 906854400 | bytes 29884416 | tf_op jit(solution)/shard_map/dot_general | solution.py:95
  90.9 0.0 copy-start.1
  90.9 0.0 copy-start.3
  90.9 0.0 copy-start.2
  90.9 14.3 %fusion.15 = bf16[32,3072]{1,0:T(8,128)(2,1)} fusion(f32[32,3072]{1,0:T(8,128)S(1)} %fusion.4, bf16[1,3072,4608]{2,1,0:T(8,128)(2,1)} %param.13, f32[32,4608]{1,0:T(8,128)S(1)} %fusion.10, f32[32,4608]{1,0:T(8,128)S(1)} %fusion, f32[32,4608]{1,0:T(8,128)S(1)} %fusion.6), kind=kOutput, calls=%fused_computation.18 | convolution fusion | flops 907640832 | bytes 30670848 | tf_op jit(solution)/shard_map/dot_general | solution.py:95
  105.2 0.0 reduce-scatter.5.cloned.1.call-update
  105.2 0.0 reduce-scatter.3.cloned.1.call-done
  105.2 5.0 %all-to-all-start.1 = ((bf16[4,8,1536]{2,1,0:T(8,128)(2,1)}), bf16[4,8,1536]{2,1,0:T(8,128)(2,1)S(1)}, u32[]{:S(2)}, u32[]{:S(2)}) async-start(bf16[4,8,1536]{2,1,0:T(8,128)(2,1)} %bitcast.72), calls=%async_computation.2 | async-start | bytes 196608 | tf_op jit(solution)/shard_map/all_to_all | solution.py:34
  110.3 0.1 copy.41
  110.3 0.1 reshape.87
  110.4 7.3 %reduce-scatter.5.cloned.1.call-done = bf16[32,1536]{1,0:T(8,128)(2,1)} async-done(((bf16[32,3072]{1,0:T(8,128)(2,1)}), bf16[32,1536]{1,0:T(8,128)(2,1)}) %reduce-scatter.5.cloned.1.call-update) | async-done | bytes 98320 | tf_op jit(solution)/shard_map/reduce_scatter | solution.py:30
  117.8 4.6 %all-to-all-start.3 = ((bf16[4,8,1536]{2,1,0:T(8,128)(2,1)}), bf16[4,8,1536]{2,1,0:T(8,128)(2,1)S(1)}, u32[]{:S(2)}, u32[]{:S(2)}) async-start(bf16[4,8,1536]{2,1,0:T(8,128)(2,1)} %bitcast.71), calls=%async_computation.5 | async-start | bytes 196608 | tf_op jit(solution)/shard_map/all_to_all | solution.py:34
  122.4 0.6 gather_fusion
  123.1 5.3 %all_gather.6 = bf16[16,2,3072]{2,0,1:T(8,128)(2,1)S(1)} all-gather(bf16[16,2,1536]{2,0,1:T(8,128)(2,1)S(1)} %copy.42), channel_id=1, replica_groups=mesh['dp'=4,'expert'=4,'tensor'=2] {'tensor'}, dimensions={2}, use_global_device_ids=true | all-gather | bytes 294912 | tf_op jit(solution)/shard_map/all_gather | solution.py:45
  128.4 0.1 fusion.27
  128.5 0.6 gather_fusion.1
  129.2 5.3 %all_gather.7 = bf16[16,2,3072]{2,1,0:T(2,128)(2,1)S(1)} all-gather(bf16[16,2,1536]{2,1,0:T(2,128)(2,1)S(1)} %reshape.112), channel_id=1, replica_groups=mesh['dp'=4,'expert'=4,'tensor'=2] {'tensor'}, dimensions={2}, use_global_device_ids=true | all-gather | bytes 294912 | tf_op jit(solution)/shard_map/all_gather | solution.py:45
  134.5 0.5 convert_reduce_fusion
  135.0 0.3 fusion.47
  135.4 0.5 fusion.38
  135.8 20.1 %all-reduce = (f32[3072,4]{0,1:T(4,128)S(1)}, f32[3072]{0:T(1024)S(1)}) all-reduce(f32[3072,4]{0,1:T(4,128)S(1)} %fusion.47, f32[3072]{0:T(1024)S(1)} %get-tuple-element.4), channel_id=1, replica_groups=mesh['dp'=4,'expert'=4,'tensor'=2] {'expert'}, use_global_device_ids=true, to_apply=%region_7.8 | all-reduce | flops 15360 | bytes 122880 | tf_op jit(solution)/shard_map/psum | solution.py:113
  156.0 11.3 %all-reduce.1 = (f32[3072,4]{0,1:T(4,128)}, f32[3072]{0:T(1024)}) all-reduce(f32[3072,4]{0,1:T(4,128)S(1)} %get-tuple-element.8, f32[3072]{0:T(1024)S(1)} %get-tuple-element.9), channel_id=1, replica_groups=mesh['dp'=4,'expert'=4,'tensor'=2] {'dp'}, use_global_device_ids=true, to_apply=%region_8.9 | all-reduce | flops 15360 | bytes 122880 | tf_op jit(solution)/shard_map/psum | solution.py:113
  167.2 0.8 fusion.35
  (19 shorter events, 0.2 us)
Async XLA Ops:
  7.2 11.0 %copy-start = (bf16[3072,4]{0,1:T(4,128)(2,1)S(1)}, bf16[3072,4]{0,1:T(4,128)(2,1)}, u32[]{:S(2)}) copy-start(bf16[3072,4]{0,1:T(4,128)(2,1)} %param.12) | copy-start | bytes 73732
  10.9 13.9 %all-to-all-start = ((bf16[4,8,3072]{2,1,0:T(8,128)(2,1)}), bf16[4,8,3072]{2,1,0:T(8,128)(2,1)S(1)}, u32[]{:S(2)}, u32[]{:S(2)}) async-start(bf16[4,8,3072]{2,1,0:T(8,128)(2,1)} %fusion.24), calls=%async_computation | async-start | bytes 393216 | tf_op jit(solution)/shard_map/all_to_all | solution.py:23
  24.8 39.0 %all-to-all-start.2 = ((bf16[4,8,3072]{2,1,0:T(8,128)(2,1)}), bf16[4,8,3072]{2,1,0:T(8,128)(2,1)S(1)}, u32[]{:S(2)}, u32[]{:S(2)}) async-start(bf16[4,8,3072]{2,1,0:T(8,128)(2,1)} %fusion.23), calls=%async_computation.3 | async-start | bytes 393216 | tf_op jit(solution)/shard_map/all_to_all | solution.py:23
  28.1 77.1 %reduce-scatter.3.cloned.1.call-start = ((), (), s32[]{:S(2)}) async-start(), calls=%async_computation.6 | async-start | bytes 294912 | tf_op jit(solution)/shard_map/reduce_scatter | solution.py:30
  63.6 54.2 %reduce-scatter.5.cloned.1.call-start = ((), (), s32[]{:S(2)}) async-start(), calls=%async_computation.7 | async-start | bytes 294912 | tf_op jit(solution)/shard_map/reduce_scatter | solution.py:30
  90.9 19.4 %copy-start.4 = (s32[16,2]{0,1:T(2,128)S(1)}, s32[16,2]{0,1:T(2,128)}, u32[]{:S(2)}) copy-start(s32[16,2]{0,1:T(2,128)} %param.16) | copy-start | bytes 388
  90.9 44.5 %copy-start.1 = (bf16[16,3072]{1,0:T(8,128)(2,1)S(1)}, bf16[16,3072]{1,0:T(8,128)(2,1)}, u32[]{:S(2)}) copy-start(bf16[16,3072]{1,0:T(8,128)(2,1)} %param.9) | copy-start | bytes 294916
  90.9 44.4 %copy-start.3 = (f32[3072]{0:T(1024)S(1)}, f32[3072]{0:T(1024)}, u32[]{:S(2)}) copy-start(f32[3072]{0:T(1024)} %param.11) | copy-start | bytes 36868
  90.9 76.3 %copy-start.2 = (bf16[16,3072]{1,0:T(8,128)(2,1)S(1)}, bf16[16,3072]{1,0:T(8,128)(2,1)}, u32[]{:S(2)}) copy-start(bf16[16,3072]{1,0:T(8,128)(2,1)} %param.10) | copy-start | bytes 294916
  105.2 12.5 %all-to-all-start.1 = ((bf16[4,8,1536]{2,1,0:T(8,128)(2,1)}), bf16[4,8,1536]{2,1,0:T(8,128)(2,1)S(1)}, u32[]{:S(2)}, u32[]{:S(2)}) async-start(bf16[4,8,1536]{2,1,0:T(8,128)(2,1)} %bitcast.72), calls=%async_computation.2 | async-start | bytes 196608 | tf_op jit(solution)/shard_map/all_to_all | solution.py:34
  117.8 10.8 %all-to-all-start.3 = ((bf16[4,8,1536]{2,1,0:T(8,128)(2,1)}), bf16[4,8,1536]{2,1,0:T(8,128)(2,1)S(1)}, u32[]{:S(2)}, u32[]{:S(2)}) async-start(bf16[4,8,1536]{2,1,0:T(8,128)(2,1)} %bitcast.71), calls=%async_computation.5 | async-start | bytes 196608 | tf_op jit(solution)/shard_map/all_to_all | solution.py:34
Sparse Core Ops, SparseCore 0:
  63.7 12.3 reduce-scatter.2
  105.3 12.3 reduce-scatter.4
